TPU v7x, 512 devices: a whole 4x8x8 slice. The times are simulated.
512 devices in a mesh: dp: 32 (over z, y_hi), tensor: 16 (over x, y_lo, core).
Axes of the slice: x: 4, y: 8 (y_hi: 4, y_lo: 2; y = y_hi * 2 + y_lo), z: 8, core: 2. Of those that a mesh axis runs over, the one named last changes fastest.
Arguments:
- tokens_in: bfloat16 [4096, 4096], P(('dp', 'tensor')), may hold values from -6 to 6
- grad_out: bfloat16 [4096, 4096], P(('dp', 'tensor')), may hold values from -6 to 6
- gate_pre: bfloat16 [4096, 7168], P('dp', 'tensor'), may hold values from -6 to 6
- up_pre: bfloat16 [4096, 7168], P('dp', 'tensor'), may hold values from -6 to 6
- gate_weight: bfloat16 [4096, 7168], P('dp', 'tensor'), may hold values from -0.09375 to 0.09375
- up_weight: bfloat16 [4096, 7168], P('dp', 'tensor'), may hold values from -0.09375 to 0.09375
- down_weight: bfloat16 [7168, 4096], P('tensor', 'dp'), may hold values from -0.0625 to 0.0625
- norm_gain: float32 [4096], replicated, may hold values from 0.1 to 1.9
Outputs:
- input_grad: bfloat16 [4096, 4096], P(('dp', 'tensor'))
- gain_grad: float32 [4096], replicated
- down_grad: bfloat16 [7168, 4096], P('tensor', 'dp')
All inputs are finite; a program needn't handle non-finite values.
Results may differ from a plain program's by a relative error of at most 0.015.
Values may be sent and summed in bfloat16 or wider, within the bound.
A program may use at most 64 MiB of HBM per device.

v0:
```python
import jax
import jax.numpy as jnp
from jax import lax
from jax.sharding import Mesh
from jax.sharding import PartitionSpec as P

Z = "dp_0"
YH = "dp_1"
TENSOR = ("tensor_0", "tensor_1", "tensor_2")
DP = ("dp_0", "dp_1")
DP_TENSOR = ("dp_0", "dp_1", "tensor_0", "tensor_1", "tensor_2")


def nt(a, b):
    return lax.dot_general(a, b, (((1,), (1,)), ((), ())), preferred_element_type=jnp.float32)


def tn(a, b):
    return lax.dot_general(a, b, (((0,), (0,)), ((), ())), preferred_element_type=jnp.float32)


def swap(x, axis):
    return lax.all_to_all(x, axis, split_axis=0, concat_axis=0, tiled=True)


def per_device(
    tokens_in, grad_out, gate_pre, up_pre, gate_weight, up_weight, down_weight, norm_gain
):
    mine = swap(grad_out.reshape(8, 8, 4, 128).transpose(2, 0, 1, 3), YH)
    rows = lax.all_gather(mine.reshape(32, 1024), TENSOR, axis=0, tiled=True)
    rows = rows.reshape(16, 4, 8, 1024).transpose(1, 0, 2, 3).reshape(512, 1024)
    down = lax.all_gather(down_weight, Z, axis=1, tiled=True)
    gate_w = lax.all_gather(gate_weight, Z, axis=0, tiled=True)
    up_w = lax.all_gather(up_weight, Z, axis=0, tiled=True)
    gate = lax.all_gather(gate_pre, YH, axis=0, tiled=True).astype(jnp.float32)
    up = lax.all_gather(up_pre, YH, axis=0, tiled=True).astype(jnp.float32)
    sig = jax.nn.sigmoid(gate)
    silu = gate * sig
    act = (silu * up).astype(jnp.bfloat16)
    part = nt(rows, down).astype(jnp.bfloat16).reshape(4, 128, 448)
    grad_act = swap(part, YH).astype(jnp.float32).sum(axis=0).astype(jnp.bfloat16)
    grad_act = lax.all_gather(grad_act, YH, axis=0, tiled=True).astype(jnp.float32)
    grad_gate = (grad_act * up * sig * (1.0 + gate * (1.0 - sig))).astype(jnp.bfloat16)
    grad_up = (grad_act * silu).astype(jnp.bfloat16)
    norm = (nt(grad_gate, gate_w) + nt(grad_up, up_w)).astype(jnp.bfloat16)
    norm = norm.reshape(4, 16, 8, 1024).transpose(1, 0, 2, 3)
    norm = swap(norm, TENSOR).astype(jnp.float32).sum(axis=0)
    norm = swap(norm, YH).reshape(4, 8, 8, 128)
    grad_norm = norm.transpose(1, 2, 0, 3).reshape(8, 4096)
    total = tn(act, rows).astype(jnp.bfloat16).reshape(448, 8, 128).transpose(1, 0, 2)
    down_grad = swap(total, Z).astype(jnp.float32).sum(axis=0).astype(jnp.bfloat16)
    inputs = tokens_in.astype(jnp.float32)
    inv_rms = lax.rsqrt(jnp.mean(inputs * inputs, axis=1, keepdims=True) + 1e-05)
    normed = inputs * inv_rms
    gain_grad = lax.psum(jnp.sum(grad_norm * normed, axis=0), DP_TENSOR)
    scaled = grad_norm * norm_gain
    inner = jnp.mean(scaled * normed, axis=1, keepdims=True)
    input_grad = (grad_out.astype(jnp.float32) + inv_rms * (scaled - normed * inner)).astype(
        jnp.bfloat16
    )
    return (input_grad, gain_grad, down_grad)


def solution(mesh):
    finer = Mesh(
        mesh.devices.reshape(8, 4, 4, 2, 2), ("dp_0", "dp_1", "tensor_0", "tensor_1", "tensor_2")
    )
    return jax.shard_map(
        per_device,
        mesh=finer,
        in_specs=(
            P(DP_TENSOR, None),
            P(DP_TENSOR, None),
            P(DP, TENSOR),
            P(DP, TENSOR),
            P(DP, TENSOR),
            P(DP, TENSOR),
            P(TENSOR, DP),
            P(),
        ),
        out_specs=(P(DP_TENSOR, None), P(), P(TENSOR, DP)),
        check_vma=False,
    )
```

profile of v0, /device:TPU:1, one launch (start us, length us, event | category | flops | bytes accessed | tf_op | source)
XLA Modules:
  0.0 346.4 jit_solution(479711068150174751)
XLA Ops:
  7.2 0.9 copy.37
  8.1 14.3 %all_to_all.25 = bf16[4,8,8,128]{3,2,1,0:T(8,128)(2,1)S(1)} all-to-all(bf16[4,8,8,128]{3,2,1,0:T(8,128)(2,1)S(1)} %bitcast.51), channel_id=1, replica_groups=mesh['dp_0'=8,'dp_1'=4,'tensor_0'=4,'tensor_1'=2,'tensor_2'=2] {'dp_1'}, dimensions={0} | all-to-all | bytes 131072 | tf_op jit(solution)/shard_map/all_to_all | solution.py:23
  23.1 28.1 %all_gather.26 = bf16[1024,448]{0,1:T(8,128)(2,1)S(1)} all-gather(bf16[128,448]{0,1:T(8,128)(2,1)} %param.12), channel_id=1, replica_groups=mesh['dp_0'=8,'dp_1'=4,'tensor_0'=4,'tensor_1'=2,'tensor_2'=2] {'dp_0'}, dimensions={0}, use_global_device_ids=true | all-gather | bytes 1032192 | tf_op jit(solution)/shard_map/all_gather | solution.py:33
  51.2 22.6 %all_gather.22 = bf16[448,1024]{1,0:T(8,128)(2,1)S(1)} all-gather(bf16[448,128]{1,0:T(8,128)(2,1)} %param.14), channel_id=1, replica_groups=mesh['dp_0'=8,'dp_1'=4,'tensor_0'=4,'tensor_1'=2,'tensor_2'=2] {'dp_0'}, dimensions={1}, use_global_device_ids=true | all-gather | bytes 1032192 | tf_op jit(solution)/shard_map/all_gather | solution.py:32
  73.7 1.3 copy.17
  75.8 0.8 copy.34
  76.6 3.5 all-to-all-start.1
  80.1 23.9 %all_gather.25 = bf16[512,448]{0,1:T(8,128)(2,1)S(1)} all-gather(bf16[128,448]{0,1:T(8,128)(2,1)S(1)} %copy-done.5), channel_id=1, replica_groups=mesh['dp_0'=8,'dp_1'=4,'tensor_0'=4,'tensor_1'=2,'tensor_2'=2] {'dp_1'}, dimensions={0}, use_global_device_ids=true | all-gather | bytes 573440 | tf_op jit(solution)/shard_map/all_gather | solution.py:35
  104.0 16.0 %all_gather.24 = bf16[512,448]{0,1:T(8,128)(2,1)S(1)} all-gather(bf16[128,448]{0,1:T(8,128)(2,1)S(1)} %copy-done.6), channel_id=1, replica_groups=mesh['dp_0'=8,'dp_1'=4,'tensor_0'=4,'tensor_1'=2,'tensor_2'=2] {'dp_1'}, dimensions={0}, use_global_device_ids=true | all-gather | bytes 573440 | tf_op jit(solution)/shard_map/all_gather | solution.py:36
  120.0 20.3 %all_gather.27 = bf16[1024,448]{0,1:T(8,128)(2,1)} all-gather(bf16[128,448]{0,1:T(8,128)(2,1)} %param.13), channel_id=1, replica_groups=mesh['dp_0'=8,'dp_1'=4,'tensor_0'=4,'tensor_1'=2,'tensor_2'=2] {'dp_0'}, dimensions={0}, use_global_device_ids=true | all-gather | bytes 1032192 | tf_op jit(solution)/shard_map/all_gather | solution.py:34
  140.4 16.1 %all_gather.23 = bf16[512,448]{0,1:T(8,128)(2,1)S(1)} all-gather(bf16[128,448]{0,1:T(8,128)(2,1)S(1)} %reduce_sum.61), channel_id=1, replica_groups=mesh['dp_0'=8,'dp_1'=4,'tensor_0'=4,'tensor_1'=2,'tensor_2'=2] {'dp_1'}, dimensions={0}, use_global_device_ids=true | all-gather | bytes 573440 | tf_op jit(solution)/shard_map/all_gather | solution.py:42
  156.6 0.9 fusion.11
  157.8 0.8 add_convert_fusion
  158.6 1.1 copy.32
  159.7 25.8 %all-to-all-start.2 = ((bf16[16,4,8,1024]{3,2,1,0:T(8,128)(2,1)}), bf16[16,4,8,1024]{3,2,1,0:T(8,128)(2,1)S(1)}, u32[]{:S(2)}, u32[]{:S(2)}) async-start(bf16[16,4,8,1024]{3,2,1,0:T(8,128)(2,1)} %bitcast.36), calls=%async_computation.2 | async-start | bytes 2097152 | tf_op jit(solution)/shard_map/all_to_all | solution.py:23
  186.2 1.1 copy.33
  187.4 13.8 %all-to-all-done.2 = bf16[16,4,8,1024]{3,2,1,0:T(8,128)(2,1)S(1)} async-done(((bf16[16,4,8,1024]{3,2,1,0:T(8,128)(2,1)}), bf16[16,4,8,1024]{3,2,1,0:T(8,128)(2,1)S(1)}, u32[]{:S(2)}, u32[]{:S(2)}) %all-to-all-start.2) | async-done | bytes 1048608 | tf_op jit(solution)/shard_map/all_to_all | solution.py:23
  201.1 4.5 %all-to-all-start.4 = ((bf16[8,448,128]{2,1,0:T(8,128)(2,1)}), bf16[8,448,128]{2,1,0:T(8,128)(2,1)S(1)}, u32[]{:S(2)}, u32[]{:S(2)}) async-start(bf16[8,448,128]{2,1,0:T(8,128)(2,1)} %bitcast.38), calls=%async_computation.4 | async-start | bytes 1835008 | tf_op jit(solution)/shard_map/all_to_all | solution.py:23
  205.8 0.8 convert_reduce_fusion
  206.6 25.4 %all-to-all-done.4 = bf16[8,448,128]{2,1,0:T(8,128)(2,1)S(1)} async-done(((bf16[8,448,128]{2,1,0:T(8,128)(2,1)}), bf16[8,448,128]{2,1,0:T(8,128)(2,1)S(1)}, u32[]{:S(2)}, u32[]{:S(2)}) %all-to-all-start.4) | async-done | bytes 917536 | tf_op jit(solution)/shard_map/all_to_all | solution.py:23
  232.0 4.0 %all-to-all-start.3 = ((f32[4,8,1024]{2,1,0:T(8,128)}), f32[4,8,1024]{2,1,0:T(8,128)S(1)}, u32[]{:S(2)}, u32[]{:S(2)}) async-start(f32[4,8,1024]{2,1,0:T(8,128)} %convert_reduce_fusion), calls=%async_computation.3 | async-start | bytes 262144 | tf_op jit(solution)/shard_map/all_to_all | solution.py:23
  236.0 0.8 reduce_sum.65
  236.8 6.6 %all-to-all-done.3 = f32[4,8,1024]{2,1,0:T(8,128)S(1)} async-done(((f32[4,8,1024]{2,1,0:T(8,128)}), f32[4,8,1024]{2,1,0:T(8,128)S(1)}, u32[]{:S(2)}, u32[]{:S(2)}) %all-to-all-start.3) | async-done | bytes 131104 | tf_op jit(solution)/shard_map/all_to_all | solution.py:23
  243.8 95.1 %psum.7 = f32[4096]{0:T(1024)} all-reduce(f32[4096]{0:T(1024)S(1)} %get-tuple-element.3), channel_id=1, replica_groups=mesh['dp_0'=8,'dp_1'=4,'tensor_0'=4,'tensor_1'=2,'tensor_2'=2] {'dp_0','..., use_global_device_ids=true, to_apply=%region_5.0 | all-reduce | flops 4096 | bytes 32768 | tf_op jit(solution)/shard_map/psum | solution.py:55
  (32 shorter events, 3.7 us)
Async XLA Ops:
  7.2 66.6 %all-gather.2.cloned.1.call-start = ((), (), s32[]{:S(2)}) async-start(), calls=%async_computation.5 | async-start | bytes 1114112 | tf_op jit(solution)/shard_map/all_gather | solution.py:30
  75.1 5.0 %copy-start.5 = (bf16[128,448]{0,1:T(8,128)(2,1)S(1)}, bf16[128,448]{0,1:T(8,128)(2,1)}, u32[]{:S(2)}) copy-start(bf16[128,448]{0,1:T(8,128)(2,1)} %param.10) | copy-start | bytes 344068
  75.7 28.2 %copy-start.6 = (bf16[128,448]{0,1:T(8,128)(2,1)S(1)}, bf16[128,448]{0,1:T(8,128)(2,1)}, u32[]{:S(2)}) copy-start(bf16[128,448]{0,1:T(8,128)(2,1)} %param.11) | copy-start | bytes 344068
  76.6 63.8 %all-to-all-start.1 = ((bf16[4,128,448]{1,2,0:T(8,128)(2,1)}), bf16[4,128,448]{1,2,0:T(8,128)(2,1)S(1)}, u32[]{:S(2)}, u32[]{:S(2)}) async-start(bf16[4,128,448]{1,2,0:T(8,128)(2,1)} %bitcast.39), calls=%async_computation.1 | async-start | bytes 917504 | tf_op jit(solution)/shard_map/all_to_all | solution.py:23
  120.0 37.5 %copy-start.2 = (bf16[512,448]{0,1:T(8,128)(2,1)}, bf16[512,448]{0,1:T(8,128)(2,1)S(1)}, u32[]{:S(2)}) copy-start(bf16[512,448]{0,1:T(8,128)(2,1)S(1)} %all_gather.24) | copy-start | bytes 1376260
  156.6 1.2 copy-start
  158.6 26.9 %copy-start.3 = (bf16[512,448]{0,1:T(8,128)(2,1)S(1)}, bf16[512,448]{0,1:T(8,128)(2,1)}, u32[]{:S(2)}) copy-start(bf16[512,448]{0,1:T(8,128)(2,1)} %copy-done.2) | copy-start | bytes 1376260
  159.7 41.5 %all-to-all-start.2 = ((bf16[16,4,8,1024]{3,2,1,0:T(8,128)(2,1)}), bf16[16,4,8,1024]{3,2,1,0:T(8,128)(2,1)S(1)}, u32[]{:S(2)}, u32[]{:S(2)}) async-start(bf16[16,4,8,1024]{3,2,1,0:T(8,128)(2,1)} %bitcast.36), calls=%async_computation.2 | async-start | bytes 2097152 | tf_op jit(solution)/shard_map/all_to_all | solution.py:23
  186.2 19.4 %copy-start.1 = (bf16[8,4096]{1,0:T(8,128)(2,1)S(1)}, bf16[8,4096]{1,0:T(8,128)(2,1)}, u32[]{:S(2)}) copy-start(bf16[8,4096]{1,0:T(8,128)(2,1)} %param.8) | copy-start | bytes 196612
  201.1 30.9 %all-to-all-start.4 = ((bf16[8,448,128]{2,1,0:T(8,128)(2,1)}), bf16[8,448,128]{2,1,0:T(8,128)(2,1)S(1)}, u32[]{:S(2)}, u32[]{:S(2)}) async-start(bf16[8,448,128]{2,1,0:T(8,128)(2,1)} %bitcast.38), calls=%async_computation.4 | async-start | bytes 1835008 | tf_op jit(solution)/shard_map/all_to_all | solution.py:23
  205.6 37.9 %copy-start.7 = (f32[4096]{0:T(1024)S(1)}, f32[4096]{0:T(1024)}, u32[]{:S(2)}) copy-start(f32[4096]{0:T(1024)} %param.15) | copy-start | bytes 49156
  205.6 133.2 %copy-start.4 = (bf16[8,4096]{1,0:T(8,128)(2,1)S(1)}, bf16[8,4096]{1,0:T(8,128)(2,1)}, u32[]{:S(2)}) copy-start(bf16[8,4096]{1,0:T(8,128)(2,1)} %param.9) | copy-start | bytes 196612
  232.0 11.4 %all-to-all-start.3 = ((f32[4,8,1024]{2,1,0:T(8,128)}), f32[4,8,1024]{2,1,0:T(8,128)S(1)}, u32[]{:S(2)}, u32[]{:S(2)}) async-start(f32[4,8,1024]{2,1,0:T(8,128)} %convert_reduce_fusion), calls=%async_computation.3 | async-start | bytes 262144 | tf_op jit(solution)/shard_map/all_to_all | solution.py:23
Sparse Core Ops, SparseCore 0:
  23.2 39.1 all-gather.1
where the time goes:
time: 347 us; the launch traced here: 346 us
  blocking collectives  236 us (68%)
  waiting for transfers between devices  45.7 us (13%)
  starting transfers between devices  37.8 us (11%)
  between operations  14.2 us (4%)
  local copies, waits for them, and re-layouts  6.3 us (2%)
    psum x1, blocking collectives, per_device(): gain_grad = lax.psum(jnp.sum(grad_norm * normed, axis=0), DP_TENSOR)  95.1 us
    all_to_all x4, waiting for transfers between devices, swap(): return lax.all_to_all(x, axis, split_axis=0, concat_axis=0, tiled=True)  45.7 us
    all_to_all x4, starting transfers between devices, swap(): return lax.all_to_all(x, axis, split_axis=0, concat_axis=0, tiled=True)  37.8 us
    all_gather x1, blocking collectives, per_device(): gate_w = lax.all_gather(gate_weight, Z, axis=0, tiled=True)  28.1 us
    all_gather x1, blocking collectives, per_device(): gate = lax.all_gather(gate_pre, YH, axis=0, tiled=True).astype(jnp.float32)  23.9 us
    all_gather x1, blocking collectives, per_device(): down = lax.all_gather(down_weight, Z, axis=1, tiled=True)  22.6 us
    all_gather x1, blocking collectives, per_device(): up_w = lax.all_gather(up_weight, Z, axis=0, tiled=True)  20.3 us
    all_gather x1, blocking collectives, per_device(): lax.all_gather(grad_act, YH, axis=0, tiled=True).astype(jnp.float32)  16.1 us
  transfers between devices with their start and end apart: 5, of which 3 were waited for; matrix products, arithmetic and copies ran while one was open for 1% of the time, Pallas kernels for 0%

commit v1 on v0

--- a/solution.py
+++ b/solution.py
@@ -52,7 +52,7 @@
     inputs = tokens_in.astype(jnp.float32)
     inv_rms = lax.rsqrt(jnp.mean(inputs * inputs, axis=1, keepdims=True) + 1e-05)
     normed = inputs * inv_rms
-    gain_grad = lax.psum(jnp.sum(grad_norm * normed, axis=0), DP_TENSOR)
+    gain_grad = jnp.sum(lax.all_gather(jnp.sum(grad_norm * normed, axis=0), DP_TENSOR), axis=0)
     scaled = grad_norm * norm_gain
     inner = jnp.mean(scaled * normed, axis=1, keepdims=True)
     input_grad = (grad_out.astype(jnp.float32) + inv_rms * (scaled - normed * inner)).astype(

time: 347 us -> 1060 us (3.05)
  waiting for transfers between devices: 45.7 us -> 809 us
  blocking collectives: 236 us -> 169 us
    all_gather x0 -> x1, waiting for transfers between devices: none -> 786 us  [per_device(): lax.all_gather(jnp.sum(grad_norm * normed, axis=0), DP_TENSOR)]
    psum x1 -> x0, blocking collectives: 95.1 us -> none  [per_device(): gain_grad = lax.psum(jnp.sum(grad_norm * normed, axis=0), DP_TENSOR)]
    all_to_all x1 -> x2, blocking collectives: 14.3 us -> 41.6 us  [swap(): return lax.all_to_all(x, axis, split_axis=0, concat_axis=0, tiled=True)]
    all_to_all x4 -> x3, waiting for transfers between devices: 45.7 us -> 22.8 us  [swap(): return lax.all_to_all(x, axis, split_axis=0, concat_axis=0, tiled=True)]
    all_to_all x4 -> x3, starting transfers between devices: 37.8 us -> 32.9 us  [swap(): return lax.all_to_all(x, axis, split_axis=0, concat_axis=0, tiled=True)]
  transfers between devices with their start and end apart: 5 -> 5, of which waited for: 3 -> 3; matrix products, arithmetic and copies ran while one was open for 1% -> 0% of each run, Pallas kernels for 0% -> 0%
where the time goes in v1:
time: 1060 us; the launch traced here: 1050 us
  waiting for transfers between devices  809 us (76%)
  blocking collectives  169 us (16%)
  starting transfers between devices  33 us (3%)
  local copies, waits for them, and re-layouts  14.7 us (1%)
  between operations  14.2 us (1%)
    all_gather x1, waiting for transfers between devices, per_device(): lax.all_gather(jnp.sum(grad_norm * normed, axis=0), DP_TENSOR)  786 us
    all_to_all x2, blocking collectives, swap(): return lax.all_to_all(x, axis, split_axis=0, concat_axis=0, tiled=True)  41.6 us
    all_to_all x3, starting transfers between devices, swap(): return lax.all_to_all(x, axis, split_axis=0, concat_axis=0, tiled=True)  32.9 us
    all_gather x1, blocking collectives, per_device(): gate_w = lax.all_gather(gate_weight, Z, axis=0, tiled=True)  28.1 us
    all_gather x1, blocking collectives, per_device(): gate = lax.all_gather(gate_pre, YH, axis=0, tiled=True).astype(jnp.float32)  23.9 us
    all_to_all x3, waiting for transfers between devices, swap(): return lax.all_to_all(x, axis, split_axis=0, concat_axis=0, tiled=True)  22.8 us
    all_gather x1, blocking collectives, per_device(): down = lax.all_gather(down_weight, Z, axis=1, tiled=True)  22.6 us
  transfers between devices with their start and end apart: 5, of which 3 were waited for; matrix products, arithmetic and copies ran while one was open for 0% of the time, Pallas kernels for 0%

profile of v1, /device:TPU:1, one launch (start us, length us, event | category | flops | bytes accessed | tf_op | source)
XLA Modules:
  0.0 1050.7 jit_solution(15447620080094260078)
XLA Ops:
  7.2 0.9 copy.43
  8.1 14.3 %all_to_all.25 = bf16[4,8,8,128]{3,2,1,0:T(8,128)(2,1)S(1)} all-to-all(bf16[4,8,8,128]{3,2,1,0:T(8,128)(2,1)S(1)} %bitcast.52), channel_id=1, replica_groups=mesh['dp_0'=8,'dp_1'=4,'tensor_0'=4,'tensor_1'=2,'tensor_2'=2] {'dp_1'}, dimensions={0} | all-to-all | bytes 131072 | tf_op jit(solution)/shard_map/all_to_all | solution.py:23
  23.1 28.1 %all_gather.32 = bf16[1024,448]{0,1:T(8,128)(2,1)S(1)} all-gather(bf16[128,448]{0,1:T(8,128)(2,1)} %param.12), channel_id=1, replica_groups=mesh['dp_0'=8,'dp_1'=4,'tensor_0'=4,'tensor_1'=2,'tensor_2'=2] {'dp_0'}, dimensions={0}, use_global_device_ids=true | all-gather | bytes 1032192 | tf_op jit(solution)/shard_map/all_gather | solution.py:33
  51.2 22.6 %all_gather.28 = bf16[448,1024]{1,0:T(8,128)(2,1)S(1)} all-gather(bf16[448,128]{1,0:T(8,128)(2,1)} %param.14), channel_id=1, replica_groups=mesh['dp_0'=8,'dp_1'=4,'tensor_0'=4,'tensor_1'=2,'tensor_2'=2] {'dp_0'}, dimensions={1}, use_global_device_ids=true | all-gather | bytes 1032192 | tf_op jit(solution)/shard_map/all_gather | solution.py:32
  73.7 1.3 copy.23
  75.8 0.9 copy.40
  76.6 3.5 all-to-all-start.1
  80.1 23.9 %all_gather.31 = bf16[512,448]{0,1:T(8,128)(2,1)S(1)} all-gather(bf16[128,448]{0,1:T(8,128)(2,1)S(1)} %copy-done.5), channel_id=1, replica_groups=mesh['dp_0'=8,'dp_1'=4,'tensor_0'=4,'tensor_1'=2,'tensor_2'=2] {'dp_1'}, dimensions={0}, use_global_device_ids=true | all-gather | bytes 573440 | tf_op jit(solution)/shard_map/all_gather | solution.py:35
  104.0 16.1 %all_gather.30 = bf16[512,448]{0,1:T(8,128)(2,1)S(1)} all-gather(bf16[128,448]{0,1:T(8,128)(2,1)S(1)} %copy-done.6), channel_id=1, replica_groups=mesh['dp_0'=8,'dp_1'=4,'tensor_0'=4,'tensor_1'=2,'tensor_2'=2] {'dp_1'}, dimensions={0}, use_global_device_ids=true | all-gather | bytes 573440 | tf_op jit(solution)/shard_map/all_gather | solution.py:36
  120.1 20.3 %all_gather.33 = bf16[1024,448]{0,1:T(8,128)(2,1)} all-gather(bf16[128,448]{0,1:T(8,128)(2,1)} %param.13), channel_id=1, replica_groups=mesh['dp_0'=8,'dp_1'=4,'tensor_0'=4,'tensor_1'=2,'tensor_2'=2] {'dp_0'}, dimensions={0}, use_global_device_ids=true | all-gather | bytes 1032192 | tf_op jit(solution)/shard_map/all_gather | solution.py:34
  140.4 16.6 %all_gather.29 = bf16[512,448]{0,1:T(8,128)(2,1)S(1)} all-gather(bf16[128,448]{0,1:T(8,128)(2,1)S(1)} %reduce_sum.70), channel_id=1, replica_groups=mesh['dp_0'=8,'dp_1'=4,'tensor_0'=4,'tensor_1'=2,'tensor_2'=2] {'dp_1'}, dimensions={0}, use_global_device_ids=true | all-gather | bytes 573440 | tf_op jit(solution)/shard_map/all_gather | solution.py:42
  157.0 0.9 fusion.11
  158.2 0.8 add_convert_fusion
  159.0 1.1 copy.38
  160.1 25.9 %all-to-all-start.2 = ((bf16[16,4,8,1024]{3,2,1,0:T(8,128)(2,1)}), bf16[16,4,8,1024]{3,2,1,0:T(8,128)(2,1)S(1)}, u32[]{:S(2)}, u32[]{:S(2)}) async-start(bf16[16,4,8,1024]{3,2,1,0:T(8,128)(2,1)} %bitcast.36), calls=%async_computation.2 | async-start | bytes 2097152 | tf_op jit(solution)/shard_map/all_to_all | solution.py:23
  186.2 15.5 %all-to-all-done.2 = bf16[16,4,8,1024]{3,2,1,0:T(8,128)(2,1)S(1)} async-done(((bf16[16,4,8,1024]{3,2,1,0:T(8,128)(2,1)}), bf16[16,4,8,1024]{3,2,1,0:T(8,128)(2,1)S(1)}, u32[]{:S(2)}, u32[]{:S(2)}) %all-to-all-start.2) | async-done | bytes 1048608 | tf_op jit(solution)/shard_map/all_to_all | solution.py:23
  201.7 0.8 convert_reduce_fusion
  202.6 3.5 all-to-all-start.3
  206.1 7.3 all-to-all-done.3
  215.3 27.3 %all_to_all.26 = bf16[8,448,128]{2,1,0:T(8,128)(2,1)S(1)} all-to-all(bf16[8,448,128]{2,1,0:T(8,128)(2,1)S(1)} %bitcast.44), channel_id=1, replica_groups=mesh['dp_0'=8,'dp_1'=4,'tensor_0'=4,'tensor_1'=2,'tensor_2'=2] {'dp_0'}, dimensions={0} | all-to-all | bytes 1835008 | tf_op jit(solution)/shard_map/all_to_all | solution.py:23
  242.6 0.8 reduce_sum.75
  244.2 785.9 %all-gather.6.cloned.1.call-done = f32[2097152]{0:T(1024)} async-done(((f32[4096]{0:T(1024)}), f32[2097152]{0:T(1024)}) %all-gather.6.cloned.1.call-update) | async-done | bytes 8388624 | tf_op jit(solution)/shard_map/all_gather | solution.py:55
  1030.1 9.4 reshape.55
  1039.5 4.4 reduce_sum.74
  (35 shorter events, 4.4 us)
Async XLA Ops:
  7.2 66.6 %all-gather.4.cloned.1.call-start = ((), (), s32[]{:S(2)}) async-start(), calls=%async_computation.5 | async-start | bytes 1114112 | tf_op jit(solution)/shard_map/all_gather | solution.py:30
  75.1 5.0 copy-start.5
  75.7 28.2 %copy-start.6 = (bf16[128,448]{0,1:T(8,128)(2,1)S(1)}, bf16[128,448]{0,1:T(8,128)(2,1)}, u32[]{:S(2)}) copy-start(bf16[128,448]{0,1:T(8,128)(2,1)} %param.11) | copy-start | bytes 344068
  76.6 63.7 %all-to-all-start.1 = ((bf16[4,128,448]{1,2,0:T(8,128)(2,1)}), bf16[4,128,448]{1,2,0:T(8,128)(2,1)S(1)}, u32[]{:S(2)}, u32[]{:S(2)}) async-start(bf16[4,128,448]{1,2,0:T(8,128)(2,1)} %bitcast.39), calls=%async_computation.1 | async-start | bytes 917504 | tf_op jit(solution)/shard_map/all_to_all | solution.py:23
  120.1 37.9 %copy-start.2 = (bf16[512,448]{0,1:T(8,128)(2,1)}, bf16[512,448]{0,1:T(8,128)(2,1)S(1)}, u32[]{:S(2)}) copy-start(bf16[512,448]{0,1:T(8,128)(2,1)S(1)} %all_gather.30) | copy-start | bytes 1376260
  157.0 1.2 copy-start
  159.0 27.0 %copy-start.1 = (bf16[8,4096]{1,0:T(8,128)(2,1)S(1)}, bf16[8,4096]{1,0:T(8,128)(2,1)}, u32[]{:S(2)}) copy-start(bf16[8,4096]{1,0:T(8,128)(2,1)} %param.8) | copy-start | bytes 196612
  160.1 53.5 %copy-start.7 = (f32[4096]{0:T(1024)S(1)}, f32[4096]{0:T(1024)}, u32[]{:S(2)}) copy-start(f32[4096]{0:T(1024)} %param.15) | copy-start | bytes 49156
  160.1 54.3 %copy-start.3 = (bf16[512,448]{0,1:T(8,128)(2,1)S(1)}, bf16[512,448]{0,1:T(8,128)(2,1)}, u32[]{:S(2)}) copy-start(bf16[512,448]{0,1:T(8,128)(2,1)} %copy-done.2) | copy-start | bytes 1376260
  160.1 41.6 %all-to-all-start.2 = ((bf16[16,4,8,1024]{3,2,1,0:T(8,128)(2,1)}), bf16[16,4,8,1024]{3,2,1,0:T(8,128)(2,1)S(1)}, u32[]{:S(2)}, u32[]{:S(2)}) async-start(bf16[16,4,8,1024]{3,2,1,0:T(8,128)(2,1)} %bitcast.36), calls=%async_computation.2 | async-start | bytes 2097152 | tf_op jit(solution)/shard_map/all_to_all | solution.py:23
  202.6 10.9 %all-to-all-start.3 = ((f32[4,8,1024]{2,1,0:T(8,128)}), f32[4,8,1024]{2,1,0:T(8,128)S(1)}, u32[]{:S(2)}, u32[]{:S(2)}) async-start(f32[4,8,1024]{2,1,0:T(8,128)} %convert_reduce_fusion), calls=%async_computation.3 | async-start | bytes 262144 | tf_op jit(solution)/shard_map/all_to_all | solution.py:23
  206.1 824.0 %all-gather.6.cloned.1.call-start = ((), (), s32[]{:S(2)}) async-start(), calls=%async_computation.6 | async-start | bytes 8404992 | tf_op jit(solution)/shard_map/all_gather | solution.py:55
  215.2 28.3 %copy-start.4 = (bf16[8,4096]{1,0:T(8,128)(2,1)S(1)}, bf16[8,4096]{1,0:T(8,128)(2,1)}, u32[]{:S(2)}) copy-start(bf16[8,4096]{1,0:T(8,128)(2,1)} %param.9) | copy-start | bytes 196612
Sparse Core Ops, SparseCore 0:
  23.2 39.1 all-gather.3
  214.5 815.5 all-gather.5
